TPU v7x, 32 devices: a whole 2x2x4 slice. The times are simulated.
32 devices in a mesh: dp: 4 (over z), expert: 4 (over x, core), shard: 2 (over y).
Axes of the slice: x: 2, y: 2, z: 4, core: 2. Of those that a mesh axis runs over, the one named last changes fastest.
Arguments:
- tokens: bfloat16 [4, 1024, 2048], P('dp', ('expert', 'shard')), may hold values from -6 to 6
- norm_gains: float32 [2, 2048], replicated, may hold values from 0.5 to 1.5
- routers: float32 [2, 2048, 4], replicated, may hold values from -0.09375 to 0.09375
- kv_weight: bfloat16 [2048, 4096], P(('dp', 'expert', 'shard')), may hold values from -0.125 to 0.125
- query_weight: bfloat16 [4, 2048, 2048], P('expert', ('dp', 'shard')), may hold values from -0.125 to 0.125
- output_weight: bfloat16 [4, 2048, 2048], P('expert', ('dp', 'shard')), may hold values from -1 to 1
- inner_weight: bfloat16 [4, 2048, 11264], P('expert', ('dp', 'shard')), may hold values from -0.125 to 0.125
- outer_weight: bfloat16 [4, 5632, 2048], P('expert', ('dp', 'shard')), may hold values from -0.078125 to 0.078125
- route_attn: int32 [4, 1024, 2], P('dp', ('expert', 'shard')), may hold values from 0 to 3, all different within a row
- route_mlp: int32 [4, 1024, 2], P('dp', ('expert', 'shard')), may hold values from 0 to 3, all different within a row
- prefix: int32 [4], P('dp'), may hold values from 102 to 512
- cotangent: bfloat16 [4, 1024, 2048], P('dp', ('expert', 'shard')), may hold values from -6 to 6
Outputs:
- output: bfloat16 [4, 1024, 2048], P('dp', ('expert', 'shard'))
- input_grad: float32 [4, 1024, 2048], P('dp', ('expert', 'shard'))
- gain_grad: float32 [2, 2048], replicated
- router_grad: float32 [2, 2048, 4], replicated
- kv_weight_grad: float32 [2048, 4096], P(('dp', 'expert', 'shard'))
- query_weight_grad: float32 [4, 2048, 2048], P('expert', ('dp', 'shard'))
- output_weight_grad: float32 [4, 2048, 2048], P('expert', ('dp', 'shard'))
- inner_weight_grad: float32 [4, 2048, 11264], P('expert', ('dp', 'shard'))
- outer_weight_grad: float32 [4, 5632, 2048], P('expert', ('dp', 'shard'))
Inputs may be any that keep to these rules, and one draw needn't show every extreme that they name: `route_attn`: each token names 2 different experts in each route array. `route_mlp`: each token names 2 different experts in each route array. Keys before a sequence's prefix length are seen by every query of that sequence.
All inputs are finite; a program needn't handle non-finite values.
Results may differ from a plain program's by a relative error of at most 0.02.
Values may be sent and summed in bfloat16 or wider, within the bound.
A program may use at most 384 MiB of HBM per device.

v0:
```python
import jax
import jax.numpy as jnp
from jax import lax
from jax.sharding import PartitionSpec as P

D = 2048
HEADS = 16
HEAD_DIM = 128
FF = 5632


eps = 1e-05
finest = lax.Precision.HIGHEST


def matmul(first, second):
    return jnp.dot(first, second, preferred_element_type=jnp.float32)


def precise(first, second):
    return jnp.dot(first, second, precision=finest, preferred_element_type=jnp.float32)


def slot_plan(routes, experts, capacity):
    pairs = routes.reshape(-1)
    onehot = (pairs[:, None] == jnp.arange(experts, dtype=jnp.int32)[None, :]).astype(jnp.int32)
    before = jnp.cumsum(onehot, axis=0) - onehot
    rank = jnp.sum(before * onehot, axis=1)
    kept = rank < capacity
    target = pairs * capacity + rank
    place = (target[None, :] == jnp.arange(experts * capacity, dtype=jnp.int32)[:, None]) & kept[
        None, :
    ]
    place = place.astype(jnp.float32)
    merged = place.reshape(experts * capacity, -1, 2).sum(axis=2)
    keep = kept.astype(jnp.float32).reshape(-1, 2)
    chosen = onehot.astype(jnp.float32).reshape(-1, 2, experts)
    return (place.astype(jnp.bfloat16), merged.astype(jnp.bfloat16), keep, chosen)


def from_slots(place, slots):
    flat = slots.reshape(place.shape[0], -1)
    return jnp.einsum("sp,sw->pw", place, flat, preferred_element_type=jnp.float32)


def gates_of(normed, router, chosen):
    logits = precise(normed.astype(jnp.float32), router)
    picked = jnp.sum(chosen * logits[:, None, :], axis=2)
    return jax.nn.softmax(picked, axis=1)


def router_back(gates, grad_gates, chosen, normed, router):
    grad_pick = gates * (grad_gates - jnp.sum(grad_gates * gates, axis=1, keepdims=True))
    grad_logit = jnp.sum(chosen * grad_pick[:, :, None], axis=1)
    router_grad = precise(normed.astype(jnp.float32).T, grad_logit)
    return (router_grad, precise(grad_logit, router.T))


def norm_back(values, factor, gain, grad_normed):
    unit = values * factor
    gain_grad = jnp.sum(grad_normed * unit, axis=0)
    grad_unit = grad_normed * gain
    grad_values = factor * (grad_unit - unit * jnp.mean(grad_unit * unit, axis=1, keepdims=True))
    return (grad_values, gain_grad)


def send_out(buffer):
    return lax.all_to_all(buffer, "expert", split_axis=0, concat_axis=0, tiled=True)


def send_back(buffer):
    return lax.all_to_all(buffer, "expert", split_axis=0, concat_axis=0, tiled=True)


def per_device(
    tokens,
    norm_gains,
    routers,
    kv_weight,
    query_weight,
    output_weight,
    inner_weight,
    outer_weight,
    route_attn,
    route_mlp,
    prefix,
    cotangent,
):
    tok_count = tokens.shape[1]
    experts = lax.axis_size("expert")
    capacity = 5 * tok_count // (2 * experts)
    qwidth = HEADS * HEAD_DIM
    scale = HEAD_DIM ** (-0.5)
    inputs = tokens[0].astype(jnp.float32)
    factor_attn = lax.rsqrt(jnp.mean(inputs * inputs, axis=1, keepdims=True) + eps)
    normed_attn = (inputs * factor_attn * norm_gains[0]).astype(jnp.bfloat16)
    kv_full = lax.all_gather(kv_weight, ("dp", "expert", "shard"), axis=0, tiled=True)
    keys_local = matmul(normed_attn, kv_full).astype(jnp.bfloat16)
    keys_all = lax.all_gather(keys_local, ("expert", "shard"), axis=0, tiled=True)
    gathered = (
        lax.all_gather(query_weight, ("dp", "shard"), axis=1, tiled=True),
        lax.all_gather(output_weight, ("dp", "shard"), axis=1, tiled=True),
        lax.all_gather(inner_weight, ("dp", "shard"), axis=1, tiled=True),
        lax.all_gather(outer_weight, ("dp", "shard"), axis=1, tiled=True),
    )
    query_full, output_full, inner_full, outer_full = (
        gathered[0][0],
        gathered[1][0],
        gathered[2][0],
        gathered[3][0],
    )
    place_attn, merged_attn, keep_attn, chosen_attn = slot_plan(route_attn[0], experts, capacity)
    gate_attn = gates_of(normed_attn, routers[0], chosen_attn)
    slots_attn = send_out(
        matmul(merged_attn, normed_attn).astype(jnp.bfloat16).reshape(experts, capacity, D)
    ).reshape(-1, D)
    query_back = send_back(
        matmul(slots_attn, query_full).astype(jnp.bfloat16).reshape(experts, capacity, qwidth)
    )
    queries = from_slots(place_attn, query_back).astype(jnp.bfloat16)
    offset = lax.axis_index(("expert", "shard")) * tok_count
    spot = offset + jnp.arange(2 * tok_count, dtype=jnp.int32) // 2
    column = jnp.arange(keys_all.shape[0], dtype=jnp.int32)
    visible = (column[None, :] <= spot[:, None]) | (column[None, :] < prefix[0])

    def head_parts(head):
        query = lax.dynamic_slice_in_dim(queries, head * HEAD_DIM, HEAD_DIM, 1)
        key = lax.dynamic_slice_in_dim(keys_all, head * HEAD_DIM, HEAD_DIM, 1)
        value = lax.dynamic_slice_in_dim(keys_all, qwidth + head * HEAD_DIM, HEAD_DIM, 1)
        return (query, key, value)

    def head_scores(query, key):
        scores = jnp.einsum("pd,kd->pk", query, key, preferred_element_type=jnp.float32) * scale
        return jnp.where(visible, scores, -jnp.inf)

    def head_forward(head):
        query, key, value = head_parts(head)
        scores = head_scores(query, key)
        highest = jnp.max(scores, axis=1, keepdims=True)
        expo = jnp.exp(scores - highest)
        total = jnp.sum(expo, axis=1, keepdims=True)
        weights = (expo / total).astype(jnp.bfloat16)
        result = jnp.dot(weights, value, preferred_element_type=jnp.float32).astype(jnp.bfloat16)
        return (result, (highest + jnp.log(total))[:, 0])

    head_outs, log_totals = lax.map(head_forward, jnp.arange(HEADS))
    attended = head_outs.transpose(1, 0, 2).reshape(-1, qwidth)
    output_slots = send_out(
        matmul(place_attn, attended).astype(jnp.bfloat16).reshape(experts, capacity, qwidth)
    ).reshape(-1, qwidth)
    attn_back = send_back(
        matmul(output_slots, output_full).astype(jnp.bfloat16).reshape(experts, capacity, D)
    )
    attn_pairs = from_slots(place_attn, attn_back).reshape(tok_count, 2, D)
    weight_attn = keep_attn * gate_attn
    hidden_state = inputs + jnp.sum(weight_attn[:, :, None] * attn_pairs, axis=1)
    factor_mlp = lax.rsqrt(jnp.mean(hidden_state * hidden_state, axis=1, keepdims=True) + eps)
    normed_mlp = (hidden_state * factor_mlp * norm_gains[1]).astype(jnp.bfloat16)
    place_mlp, merged_mlp, keep_mlp, chosen_mlp = slot_plan(route_mlp[0], experts, capacity)
    gate_mlp = gates_of(normed_mlp, routers[1], chosen_mlp)
    slots_mlp = send_out(
        matmul(merged_mlp, normed_mlp).astype(jnp.bfloat16).reshape(experts, capacity, D)
    ).reshape(-1, D)
    gate_up = matmul(slots_mlp, inner_full)
    gate_part = gate_up[:, :FF]
    up_part = gate_up[:, FF:]
    activated = jax.nn.silu(gate_part)
    inner = (activated * up_part).astype(jnp.bfloat16)
    mlp_back = send_back(
        matmul(inner, outer_full).astype(jnp.bfloat16).reshape(experts, capacity, D)
    )
    mlp_pairs = from_slots(place_mlp, mlp_back).reshape(tok_count, 2, D)
    weight_mlp = keep_mlp * gate_mlp
    result = hidden_state + jnp.sum(weight_mlp[:, :, None] * mlp_pairs, axis=1)
    output = result.astype(jnp.bfloat16)[None]
    regathered = (
        lax.all_gather(query_weight, ("dp", "shard"), axis=1, tiled=True),
        lax.all_gather(output_weight, ("dp", "shard"), axis=1, tiled=True),
        lax.all_gather(inner_weight, ("dp", "shard"), axis=1, tiled=True),
        lax.all_gather(outer_weight, ("dp", "shard"), axis=1, tiled=True),
    )
    query_full, output_full, inner_full, outer_full = (
        regathered[0][0],
        regathered[1][0],
        regathered[2][0],
        regathered[3][0],
    )
    grad = cotangent[0].astype(jnp.float32)
    grad_gate_mlp = keep_mlp * jnp.sum(grad[:, None, :] * mlp_pairs, axis=2)
    grad_mlp_pairs = (weight_mlp[:, :, None] * grad[:, None, :]).astype(jnp.bfloat16).reshape(-1, D)
    grad_mlp_slots = send_out(
        matmul(place_mlp, grad_mlp_pairs).astype(jnp.bfloat16).reshape(experts, capacity, D)
    ).reshape(-1, D)
    grad_inner = jnp.einsum(
        "rd,fd->rf", grad_mlp_slots, outer_full, preferred_element_type=jnp.float32
    )
    sigmoid_gate = jax.nn.sigmoid(gate_part)
    grad_gate = grad_inner * up_part * (sigmoid_gate * (1.0 + gate_part * (1.0 - sigmoid_gate)))
    grad_up = grad_inner * activated
    grad_gate_up = jnp.concatenate([grad_gate, grad_up], axis=1).astype(jnp.bfloat16)
    grad_row_mlp = send_back(
        jnp.einsum("rf,df->rd", grad_gate_up, inner_full, preferred_element_type=jnp.float32)
        .astype(jnp.bfloat16)
        .reshape(experts, capacity, D)
    )
    piece = inner
    outer_grad = lax.psum_scatter(
        jnp.einsum("rf,rd->fd", piece, grad_mlp_slots, preferred_element_type=jnp.float32).astype(
            jnp.bfloat16
        ),
        ("dp", "shard"),
        scatter_dimension=0,
        tiled=True,
    ).astype(jnp.float32)
    piece = slots_mlp
    inner_grad = lax.psum_scatter(
        jnp.einsum("rd,rf->df", piece, grad_gate_up, preferred_element_type=jnp.float32).astype(
            jnp.bfloat16
        ),
        ("dp", "shard"),
        scatter_dimension=0,
        tiled=True,
    ).astype(jnp.float32)
    grad_normed_mlp = from_slots(merged_mlp, grad_row_mlp)
    router_grad_mlp, router_part_mlp = router_back(
        gate_mlp, grad_gate_mlp, chosen_mlp, normed_mlp, routers[1]
    )
    grad_normed_mlp = grad_normed_mlp + router_part_mlp
    grad_hidden, gain_grad_mlp = norm_back(hidden_state, factor_mlp, norm_gains[1], grad_normed_mlp)
    grad_hidden = grad_hidden + grad
    grad_gate_attn = keep_attn * jnp.sum(grad_hidden[:, None, :] * attn_pairs, axis=2)
    grad_attn_pairs = (
        (weight_attn[:, :, None] * grad_hidden[:, None, :]).astype(jnp.bfloat16).reshape(-1, D)
    )
    grad_attn_slots = send_out(
        matmul(place_attn, grad_attn_pairs).astype(jnp.bfloat16).reshape(experts, capacity, D)
    ).reshape(-1, D)
    grad_out_back = send_back(
        jnp.einsum("rd,qd->rq", grad_attn_slots, output_full, preferred_element_type=jnp.float32)
        .astype(jnp.bfloat16)
        .reshape(experts, capacity, qwidth)
    )
    grad_attended = from_slots(place_attn, grad_out_back).astype(jnp.bfloat16)
    output_grad_term = jnp.einsum(
        "rq,rd->qd", output_slots, grad_attn_slots, preferred_element_type=jnp.float32
    )
    seq_len = keys_all.shape[0]

    def head_backward(carry, head):
        kv_terms, query_terms = carry
        query, key, value = head_parts(head)
        upstream = lax.dynamic_slice_in_dim(grad_attended, head * HEAD_DIM, HEAD_DIM, 1)
        log_total = lax.dynamic_index_in_dim(log_totals, head, 0, keepdims=False)
        probs = jnp.exp(head_scores(query, key) - log_total[:, None])
        grad_probs = jnp.einsum("pd,kd->pk", upstream, value, preferred_element_type=jnp.float32)
        delta = jnp.sum(grad_probs * probs, axis=1, keepdims=True)
        grad_scores = (probs * (grad_probs - delta)).astype(jnp.bfloat16)
        grad_query = jnp.dot(grad_scores, key, preferred_element_type=jnp.float32) * scale
        grad_key = (
            jnp.einsum("pk,pd->kd", grad_scores, query, preferred_element_type=jnp.float32) * scale
        )
        grad_value = jnp.einsum(
            "pk,pd->kd", probs.astype(jnp.bfloat16), upstream, preferred_element_type=jnp.float32
        )
        kv_terms = lax.dynamic_update_slice_in_dim(kv_terms, grad_key, head * HEAD_DIM, 1)
        kv_terms = lax.dynamic_update_slice_in_dim(
            kv_terms, grad_value, qwidth + head * HEAD_DIM, 1
        )
        query_terms = lax.dynamic_update_slice_in_dim(query_terms, grad_query, head * HEAD_DIM, 1)
        return ((kv_terms, query_terms), None)

    start_carry = (
        jnp.zeros((seq_len, 2 * qwidth), jnp.float32),
        jnp.zeros((2 * tok_count, qwidth), jnp.float32),
    )
    (grad_kv_terms, grad_query_terms), unused = lax.scan(
        head_backward, start_carry, jnp.arange(HEADS)
    )
    grad_queries = grad_query_terms.astype(jnp.bfloat16)
    grad_keys = lax.psum_scatter(
        grad_kv_terms.astype(jnp.bfloat16), ("expert", "shard"), scatter_dimension=0, tiled=True
    )
    grad_query_slots = send_out(
        matmul(place_attn, grad_queries).astype(jnp.bfloat16).reshape(experts, capacity, qwidth)
    ).reshape(-1, qwidth)
    grad_row_attn = send_back(
        jnp.einsum("rq,dq->rd", grad_query_slots, query_full, preferred_element_type=jnp.float32)
        .astype(jnp.bfloat16)
        .reshape(experts, capacity, D)
    )
    query_grad_term = jnp.einsum(
        "rd,rq->dq", slots_attn, grad_query_slots, preferred_element_type=jnp.float32
    )
    query_grad, output_grad = (
        lax.psum_scatter(
            query_grad_term.astype(jnp.bfloat16), ("dp", "shard"), scatter_dimension=0, tiled=True
        ).astype(jnp.float32),
        lax.psum_scatter(
            output_grad_term.astype(jnp.bfloat16), ("dp", "shard"), scatter_dimension=0, tiled=True
        ).astype(jnp.float32),
    )
    piece = normed_attn
    kv_grad = lax.psum_scatter(
        jnp.einsum("td,tk->dk", piece, grad_keys, preferred_element_type=jnp.float32),
        ("dp", "expert", "shard"),
        scatter_dimension=0,
        tiled=True,
    )
    grad_normed_attn = from_slots(merged_attn, grad_row_attn)
    grad_normed_attn = grad_normed_attn + jnp.einsum(
        "tk,dk->td", grad_keys, kv_full, preferred_element_type=jnp.float32
    )
    router_grad_attn, router_part_attn = router_back(
        gate_attn, grad_gate_attn, chosen_attn, normed_attn, routers[0]
    )
    grad_normed_attn = grad_normed_attn + router_part_attn
    grad_inputs, gain_grad_attn = norm_back(inputs, factor_attn, norm_gains[0], grad_normed_attn)
    grad_inputs = grad_inputs + grad_hidden
    gain_grad, router_grad = lax.psum(
        (
            jnp.stack([gain_grad_attn, gain_grad_mlp]),
            jnp.stack([router_grad_attn, router_grad_mlp]),
        ),
        ("dp", "expert", "shard"),
    )
    return (
        output,
        grad_inputs[None],
        gain_grad,
        router_grad,
        kv_grad,
        query_grad[None],
        output_grad[None],
        inner_grad[None],
        outer_grad[None],
    )


def solution(mesh):
    return jax.shard_map(
        per_device,
        mesh=mesh,
        in_specs=(
            P("dp", ("expert", "shard"), None),
            P(),
            P(),
            P(("dp", "expert", "shard"), None),
            P("expert", ("dp", "shard"), None),
            P("expert", ("dp", "shard"), None),
            P("expert", ("dp", "shard"), None),
            P("expert", ("dp", "shard"), None),
            P("dp", ("expert", "shard"), None),
            P("dp", ("expert", "shard"), None),
            P("dp"),
            P("dp", ("expert", "shard"), None),
        ),
        out_specs=(
            P("dp", ("expert", "shard"), None),
            P("dp", ("expert", "shard"), None),
            P(),
            P(),
            P(("dp", "expert", "shard"), None),
            P("expert", ("dp", "shard"), None),
            P("expert", ("dp", "shard"), None),
            P("expert", ("dp", "shard"), None),
            P("expert", ("dp", "shard"), None),
        ),
        check_vma=False,
    )
```

profile of v0, /device:TPU:0, one launch (start us, length us, event | category | flops | bytes accessed | tf_op | source)
XLA Modules:
  0.0 4437.4 jit_solution(1781969885716199297)
XLA Ops:
  10.8 117.2 %all-gather.9.cloned.1.call-done = bf16[2048,4096]{1,0:T(8,128)(2,1)} async-done(((bf16[64,4096]{1,0:T(8,128)(2,1)}), bf16[2048,4096]{1,0:T(8,128)(2,1)}) %all-gather.9.cloned.1.call-update) | async-done | bytes 16777232 | tf_op jit(solution)/shard_map/all_gather | solution.py:97
  128.0 9.4 convolution_convert_fusion.3
  142.9 19.7 all_to_all.60
  162.6 90.2 %all-gather.7.cloned.1.call-done = bf16[1,2048,2048]{2,1,0:T(8,128)(2,1)} async-done(((bf16[1,256,2048]{2,1,0:T(8,128)(2,1)}), bf16[1,2048,2048]{2,1,0:T(8,128)(2,1)}) %all-gather.7.cloned.1.call-update) | async-done | bytes 8388624 | tf_op jit(solution)/shard_map/all_gather | solution.py:101
  252.8 7.3 fusion.50
  264.7 24.5 all-to-all-done.1
  291.0 27.7 all-gather.11.cloned.1.call-done
  318.6 83.1 %while.30 = (s32[]{:T(128)}, bf16[16,256,128]{1,2,0:T(8,128)(2,1)}, f32[16,256]{1,0:T(8,128)S(1)}, s32[16]{0:T(128)S(1)}, bf16[256,2048]{1,0:T(8,128)(2,1)}, /*i...) while((s32[]{:T(128)}, bf16[16,256,128]{1,2,0:T(8,128)(2,1)}, ...), condition=%wide.region_11.12_spmd.clone, body=%wide.region_8.11_spmd.clone.sunk | while | flops 136871680 | bytes 4075798 | solution.py:146
  408.1 37.0 all-gather.13.cloned.1.call-done
  445.1 7.8 fusion.56
  452.9 3.9 all-to-all-start.3
  459.1 14.9 all-to-all-done.3
  478.9 4.3 all-to-all-start.4
  493.0 7.5 all-to-all-done.4
  504.1 814.2 %all-gather.15.cloned.1.call-done = bf16[1,2048,11264]{2,1,0:T(8,128)(2,1)} async-done(((bf16[1,256,11264]{2,1,0:T(8,128)(2,1)}), bf16[1,2048,11264]{2,1,0:T(8,128)(2,1)}) %all-gather.15.cloned.1.call-update) | async-done | bytes 46137360 | tf_op jit(solution)/shard_map/all_gather | solution.py:103
  1318.3 26.9 fusion.35
  1345.3 415.5 %all-gather.17.cloned.1.call-done = bf16[1,5632,2048]{2,1,0:T(8,128)(2,1)} async-done(((bf16[1,704,2048]{2,1,0:T(8,128)(2,1)}), bf16[1,5632,2048]{2,1,0:T(8,128)(2,1)}) %all-gather.17.cloned.1.call-update) | async-done | bytes 23068688 | tf_op jit(solution)/shard_map/all_gather | solution.py:104
  1760.8 27.2 multiply_convert_fusion.2
  1788.0 23.1 fusion.65
  1811.1 3.7 all-to-all-start.7
  1814.8 13.9 fusion.62
  1832.0 4.3 all-to-all-start.5
  1837.8 15.8 all-to-all-done.5
  1861.2 3.6 mul.433
  1867.0 19.7 all_to_all.61
  1886.7 7.8 fusion.59
  1898.3 16.9 all-to-all-done.9
  1917.0 4.4 broadcast_in_dim.101
  1922.5 191.7 %while.31 = (s32[]{:T(128)}, bf16[1024,4096]{1,0:T(8,128)(2,1)}, bf16[256,2048]{1,0:T(8,128)(2,1)}, s32[16]{0:T(128)S(1)}, bf16[256,2048]{1,0:T(8,128)(2,1)}, /*...) while((s32[]{:T(128)}, bf16[1024,4096]{1,0:T(8,128)(2,1)}, ...), condition=%wide.region_28.29_spmd.clone, body=%wide.region_26.28_spmd.clone.sunk | while | flops 338591488 | bytes 10100072 | solution.py:276
  2115.6 8.5 bitcast_convert_fusion
  2125.9 24.9 all_to_all.62
  2151.9 6.8 bitcast_convert_fusion.1
  2160.0 17.5 convolution_convert_fusion.2
  2177.9 31.6 convolution_convert_fusion.1
  2213.5 14.7 fusion.156
  2231.6 7.6 fusion.53
  2239.2 4.4 all-to-all-start.11
  2243.7 12.5 fusion.166
  2256.2 4.8 all-to-all-done.11
  2264.4 39.8 psum.14
  2305.5 35.1 reduce-scatter.15.cloned.1.call-done
  2343.4 147.4 %reduce-scatter.13.cloned.1.call-done = bf16[256,2048]{1,0:T(8,128)(2,1)} async-done(((bf16[2048,2048]{1,0:T(8,128)(2,1)}), bf16[256,2048]{1,0:T(8,128)(2,1)}) %reduce-scatter.13.cloned.1.call-update) | async-done | bytes 1048592 | tf_op jit(solution)/shard_map/reduce_scatter | solution.py:295
  2493.6 373.0 %reduce-scatter.17.cloned.1.call-done = bf16[704,2048]{1,0:T(8,128)(2,1)} async-done(((bf16[5632,2048]{1,0:T(8,128)(2,1)}), bf16[704,2048]{1,0:T(8,128)(2,1)}) %reduce-scatter.17.cloned.1.call-update) | async-done | bytes 2883600 | tf_op jit(solution)/shard_map/reduce_scatter | solution.py:207
  2866.6 5.1 bitcast_convert_fusion.3
  2871.7 722.8 %reduce-scatter.19.cloned.1.call-done = bf16[256,11264]{1,0:T(8,128)(2,1)} async-done(((bf16[2048,11264]{1,0:T(8,128)(2,1)}), bf16[256,11264]{1,0:T(8,128)(2,1)}) %reduce-scatter.19.cloned.1.call-update) | async-done | bytes 5767184
  3594.5 8.4 bitcast_convert_fusion.2
  3602.9 116.1 %all-reduce.3.cloned.1.call-done = f32[2,2048,4]{1,2,0:T(4,128)} async-done(((f32[2,2048,4]{1,2,0:T(4,128)}), f32[2,2048,4]{1,2,0:T(4,128)}) %all-reduce.3.cloned.1.call-update) | async-done | bytes 65552 | tf_op jit(solution)/shard_map/psum | solution.py:319
  3719.1 710.1 %reduce-scatter.11.cloned.1.call-done = f32[64,4096]{1,0:T(8,128)} async-done(((f32[2048,4096]{1,0:T(8,128)}), f32[64,4096]{1,0:T(8,128)}) %reduce-scatter.11.cloned.1.call-update) | async-done | bytes 1048592 | tf_op jit(solution)/shard_map/reduce_scatter | solution.py:303
  (459 shorter events, 308.7 us)
Async XLA Ops:
  7.2 120.8 %all-gather.9.cloned.1.call-start = ((), (), s32[]{:S(2)}) async-start(), calls=%async_computation.19 | async-start | bytes 17301504 | tf_op jit(solution)/shard_map/all_gather | solution.py:97
  7.9 244.9 %all-gather.7.cloned.1.call-start = ((), (), s32[]{:S(2)}) async-start(), calls=%async_computation.18 | async-start | bytes 9437184 | tf_op jit(solution)/shard_map/all_gather | solution.py:101
  8.7 310.0 %all-gather.11.cloned.1.call-start = ((), (), s32[]{:S(2)}) async-start(), calls=%async_computation.20 | async-start | bytes 9437184 | tf_op jit(solution)/shard_map/all_gather | solution.py:99
  9.9 132.4 %copy-start.24 = (f32[128]{0:T(128)}, f32[128]{0:T(128)S(1)}, u32[]{:S(2)}) copy-start(f32[128]{0:T(128)S(1)} %add_rsqrt_fusion.1) | copy-start | bytes 1540
  10.8 131.5 %copy-start.18 = (f32[1,2048]{1,0:T(1,128)}, f32[1,2048]{1,0:T(1,128)S(1)}, u32[]{:S(2)}) copy-start(f32[1,2048]{1,0:T(1,128)S(1)} %get-tuple-element.323) | copy-start | bytes 24580
  137.4 307.7 %all-gather.13.cloned.1.call-start = ((), (), s32[]{:S(2)}) async-start(), calls=%async_computation.21 | async-start | bytes 9437184 | tf_op jit(solution)/shard_map/all_gather | solution.py:102
  138.0 1180.4 %all-gather.15.cloned.1.call-start = ((), (), s32[]{:S(2)}) async-start(), calls=%async_computation.22 | async-start | bytes 51904512 | tf_op jit(solution)/shard_map/all_gather | solution.py:103
  138.6 2.9 copy-start
  138.6 2.9 copy-start.22
  138.6 1622.2 %all-gather.17.cloned.1.call-start = ((), (), s32[]{:S(2)}) async-start(), calls=%async_computation.23 | async-start | bytes 25952256 | tf_op jit(solution)/shard_map/all_gather | solution.py:104
  142.2 121.6 %copy-start.29 = (f32[128,2]{0,1:T(2,128)}, f32[128,2]{0,1:T(2,128)S(1)}, u32[]{:S(2)}) copy-start(f32[128,2]{0,1:T(2,128)S(1)} %get-tuple-element.313) | copy-start | bytes 3076
  142.2 331.8 %copy-start.31 = (pred[128,2]{0,1:T(4,128)(4,1)}, pred[128,2]{0,1:T(4,128)(4,1)S(1)}, u32[]{:S(2)}) copy-start(pred[128,2]{0,1:T(4,128)(4,1)S(1)} %get-tuple-element.314) | copy-start | bytes 772
  142.3 117.8 %copy-start.20 = (bf16[320,128]{1,0:T(8,128)(2,1)}, bf16[320,128]{1,0:T(8,128)(2,1)S(1)}, u32[]{:S(2)}) copy-start(bf16[320,128]{1,0:T(8,128)(2,1)S(1)} %convert_reduce_fusion.1) | copy-start | bytes 245764
  162.6 97.5 %copy-start.9 = (bf16[4,80,2048]{2,1,0:T(8,128)(2,1)}, bf16[4,80,2048]{2,1,0:T(8,128)(2,1)S(1)}, u32[]{:S(2)}) copy-start(bf16[4,80,2048]{2,1,0:T(8,128)(2,1)S(1)} %all_to_all.60) | copy-start | bytes 3932164
  260.1 29.1 all-to-all-start.1
  401.7 51.2 %copy-start.33 = (pred[1024]{0:T(1024)(128)(4,1)}, pred[1024]{0:T(1024)(128)(4,1)S(1)}, u32[]{:S(2)}) copy-start(pred[1024]{0:T(1024)(128)(4,1)S(1)} %get-tuple-element.621) | copy-start | bytes 3076
  404.6 40.6 all-to-all-start.2
  445.1 7.8 copy-start.11
  445.1 11.7 copy-start.26
  452.9 21.1 all-to-all-start.3
  477.2 6.1 copy-start.7
  478.9 21.6 all-to-all-start.4
  500.5 1260.2 %all-to-all-start.6 = ((bf16[4,80,2048]{2,1,0:T(8,128)(2,1)}), bf16[4,80,2048]{2,1,0:T(8,128)(2,1)S(1)}, u32[]{:S(2)}, u32[]{:S(2)}) async-start(bf16[4,80,2048]{2,1,0:T(8,128)(2,1)} %bitcast.39), calls=%async_computation.6 | async-start | bytes 2621440 | tf_op jit(solution)/shard_map/all_to_all | solution.py:68
  1760.8 27.2 copy-start.13
  1811.1 20.9 all-to-all-start.7
  1832.0 21.6 all-to-all-start.5
  1837.7 19.2 copy-start.5
  1837.8 19.2 copy-start.23
  1853.6 4.7 copy-start.8
  1886.7 7.8 copy-start.15
  1894.5 20.8 all-to-all-start.9
  1898.1 315.4 %reduce-scatter.9.cloned.1.call-start = ((), (), s32[]{:S(2)}) async-start(), calls=%async_computation.24 | async-start | bytes 9437184 | tf_op jit(solution)/shard_map/reduce_scatter | solution.py:280
  1917.0 5.5 copy-start.34
  2114.3 226.3 %reduce-scatter.15.cloned.1.call-start = ((), (), s32[]{:S(2)}) async-start(), calls=%async_computation.28 | async-start | bytes 9437184 | tf_op jit(solution)/shard_map/reduce_scatter | solution.py:298
  2124.1 366.7 %reduce-scatter.13.cloned.1.call-start = ((), (), s32[]{:S(2)}) async-start(), calls=%async_computation.27 | async-start | bytes 9437184 | tf_op jit(solution)/shard_map/reduce_scatter | solution.py:295
  2124.1 27.7 copy-start.10
  2158.7 707.9 %reduce-scatter.17.cloned.1.call-start = ((), (), s32[]{:S(2)}) async-start(), calls=%async_computation.29 | async-start | bytes 25952256 | tf_op jit(solution)/shard_map/reduce_scatter | solution.py:207
  2177.5 1417.0 %reduce-scatter.19.cloned.1.call-start = ((), (), s32[]{:S(2)}) async-start(), calls=%async_computation.30 | async-start | bytes 51904512
  2209.6 2.1 copy-start.28
  2209.6 2.1 copy-start.1
  2209.6 2.1 copy-start.19
  2209.6 2.1 copy-start.25
  2209.6 1509.4 %all-reduce.3.cloned.1.call-start = ((), (), s32[]{:S(2)}) async-start(), calls=%async_computation.25 | async-start | bytes 131072 | tf_op jit(solution)/shard_map/psum | solution.py:319
  2213.2 2215.9 %reduce-scatter.11.cloned.1.call-start = ((), (), s32[]{:S(2)}) async-start(), calls=%async_computation.26 | async-start | bytes 34603008 | tf_op jit(solution)/shard_map/reduce_scatter | solution.py:303
  2228.2 3.5 copy-start.17
  2239.2 4.4 copy-start.4
  2239.2 21.7 all-to-all-start.11
  2243.7 17.3 copy-start.21
  (9 other events, 12.0 us)
Sparse Core Ops, SparseCore 0:
  10.9 117.0 all-gather.8
  130.1 122.6 all-gather.6
  255.3 63.2 all-gather.10
  320.6 124.4 all-gather.12
  446.5 871.7 all-gather.14
  1319.7 441.0 all-gather.16
  2114.4 74.3 reduce-scatter.8
  2192.5 148.0 reduce-scatter.14
  2344.2 146.5 reduce-scatter.12
  2494.5 372.0 reduce-scatter.16
  2870.5 723.9 reduce-scatter.18
  3600.5 118.5 all-reduce.2
  3721.9 707.1 reduce-scatter.10
where the time goes:
time: 4450 us; the launch traced here: 4440 us
  waiting for transfers between devices  3700 us (83%)
  matrix products  432 us (10%)
  blocking collectives  104 us (2%)
  local copies, waits for them, and re-layouts  59.9 us (1%)
  loops' own time  53.5 us (1%)
    all_gather x1, waiting for transfers between devices, per_device(): lax.all_gather(inner_weight, ('dp', 'shard'), axis=1, tiled=True)  814 us
    unnamed x14, waiting for transfers between devices  726 us
    reduce_scatter x1, waiting for transfers between devices, per_device(): lax.psum_scatter(jnp.einsum('td,tk->dk', piece, grad_keys, preferred_elem...  710 us
    all_gather x1, waiting for transfers between devices, per_device(): lax.all_gather(outer_weight, ('dp', 'shard'), axis=1, tiled=True)  416 us
    reduce_scatter x1, waiting for transfers between devices, per_device(): lax.psum_scatter(jnp.einsum('rf,rd->fd', piece, grad_mlp_slots, preferred...  373 us
    reduce_scatter x1, waiting for transfers between devices, per_device(): lax.psum_scatter(query_grad_term.astype(jnp.bfloat16), ('dp', 'shard'), s...  147 us
    all_gather x1, waiting for transfers between devices, per_device(): lax.all_gather(kv_weight, ('dp', 'expert', 'shard'), axis=0, tiled=True)  117 us
    psum x1, waiting for transfers between devices, per_device(): lax.psum((jnp.stack([gain_grad_attn, gain_grad_mlp]), jnp.stack([router_g...  116 us
  transfers between devices with their start and end apart: 22, of which 19 were waited for; matrix products, arithmetic and copies ran while one was open for 7% of the time, Pallas kernels for 0%

commit v1 on v0

--- a/solution.py
+++ b/solution.py
@@ -1,24 +1,50 @@
+import functools
+
 import jax
 import jax.numpy as jnp
 from jax import lax
+from jax.experimental import pallas as pl
+from jax.experimental.pallas import tpu as pltpu
 from jax.sharding import PartitionSpec as P
 
 D = 2048
 HEADS = 16
 HEAD_DIM = 128
 FF = 5632
-
+F32 = jnp.float32
+BF16 = jnp.bfloat16
 
 eps = 1e-05
 finest = lax.Precision.HIGHEST
 
 
 def matmul(first, second):
-    return jnp.dot(first, second, preferred_element_type=jnp.float32)
+    return jnp.dot(first, second, preferred_element_type=F32)
 
 
 def precise(first, second):
-    return jnp.dot(first, second, precision=finest, preferred_element_type=jnp.float32)
+    return jnp.dot(first, second, precision=finest, preferred_element_type=F32)
+
+
+def router_back(gates, grad_gates, chosen, normed, router):
+    grad_pick = gates * (grad_gates - jnp.sum(grad_gates * gates, axis=1, keepdims=True))
+    grad_logit = jnp.sum(chosen * grad_pick[:, :, None], axis=1)
+    router_grad = precise(normed.astype(F32).T, grad_logit)
+    return (router_grad, precise(grad_logit, router.T))
+
+
+def norm_back(values, factor, gain, grad_normed):
+    unit = values * factor
+    gain_grad = jnp.sum(grad_normed * unit, axis=0)
+    grad_unit = grad_normed * gain
+    grad_values = factor * (grad_unit - unit * jnp.mean(grad_unit * unit, axis=1, keepdims=True))
+    return (grad_values, gain_grad)
+
+
+def gates_of(normed, router, chosen):
+    logits = precise(normed.astype(F32), router)
+    picked = jnp.sum(chosen * logits[:, None, :], axis=2)
+    return jax.nn.softmax(picked, axis=1)
 
 
 def slot_plan(routes, experts, capacity):
@@ -43,27 +69,6 @@
     return jnp.einsum("sp,sw->pw", place, flat, preferred_element_type=jnp.float32)
 
 
-def gates_of(normed, router, chosen):
-    logits = precise(normed.astype(jnp.float32), router)
-    picked = jnp.sum(chosen * logits[:, None, :], axis=2)
-    return jax.nn.softmax(picked, axis=1)
-
-
-def router_back(gates, grad_gates, chosen, normed, router):
-    grad_pick = gates * (grad_gates - jnp.sum(grad_gates * gates, axis=1, keepdims=True))
-    grad_logit = jnp.sum(chosen * grad_pick[:, :, None], axis=1)
-    router_grad = precise(normed.astype(jnp.float32).T, grad_logit)
-    return (router_grad, precise(grad_logit, router.T))
-
-
-def norm_back(values, factor, gain, grad_normed):
-    unit = values * factor
-    gain_grad = jnp.sum(grad_normed * unit, axis=0)
-    grad_unit = grad_normed * gain
-    grad_values = factor * (grad_unit - unit * jnp.mean(grad_unit * unit, axis=1, keepdims=True))
-    return (grad_values, gain_grad)
-
-
 def send_out(buffer):
     return lax.all_to_all(buffer, "expert", split_axis=0, concat_axis=0, tiled=True)
 
@@ -72,7 +77,365 @@
     return lax.all_to_all(buffer, "expert", split_axis=0, concat_axis=0, tiled=True)
 
 
+def exclusive_count(flags):
+    size = flags.shape[-1]
+    earlier = jnp.arange(size)[:, None] < jnp.arange(size)[None, :]
+    return jnp.dot(flags.astype(BF16), earlier.astype(BF16), preferred_element_type=F32)
+
+
+Q_ROWS = 256
+
+
+def head_mask(tile, rows, tokens, keys, prefix):
+    first = lax.rem(tile * rows, tokens)
+    spot = first + lax.broadcasted_iota(jnp.int32, (rows, keys), 0)
+    column = lax.broadcasted_iota(jnp.int32, (rows, keys), 1)
+    return (column <= spot) | (column < prefix)
+
+
+def attend_kernel(tokens, prefix_ref, q_ref, k_ref, v_ref, out_ref, lse_ref):
+    tile = pl.program_id(1)
+    rows, keys = q_ref.shape[0], k_ref.shape[0]
+    scores = lax.dot_general(q_ref[...], k_ref[...], (((1,), (1,)), ((), ())), preferred_element_type=F32)
+    scores = scores * (HEAD_DIM ** (-0.5))
+    scores = jnp.where(head_mask(tile, rows, tokens, keys, prefix_ref[0]), scores, -jnp.inf)
+    highest = jnp.max(scores, axis=1, keepdims=True)
+    expo = jnp.exp(scores - highest)
+    total = jnp.sum(expo, axis=1, keepdims=True)
+    weights = (expo / total).astype(BF16)
+    out_ref[...] = jnp.dot(weights, v_ref[...], preferred_element_type=F32).astype(BF16)
+    lse_ref[0] = highest + jnp.log(total)
+
+
+def attend(prefix, queries, keys, values):
+    pairs, width = queries.shape
+    seq = keys.shape[0]
+    heads = width // HEAD_DIM
+    tiles = pairs // Q_ROWS
+    return pl.pallas_call(
+        functools.partial(attend_kernel, pairs // 2),
+        out_shape=(
+            jax.ShapeDtypeStruct((pairs, width), BF16),
+            jax.ShapeDtypeStruct((heads, pairs, 1), F32),
+        ),
+        grid_spec=pltpu.PrefetchScalarGridSpec(
+            num_scalar_prefetch=1,
+            grid=(heads, tiles),
+            in_specs=[
+                pl.BlockSpec((Q_ROWS, HEAD_DIM), lambda h, i, p: (i, h)),
+                pl.BlockSpec((seq, HEAD_DIM), lambda h, i, p: (0, h)),
+                pl.BlockSpec((seq, HEAD_DIM), lambda h, i, p: (0, h)),
+            ],
+            out_specs=[
+                pl.BlockSpec((Q_ROWS, HEAD_DIM), lambda h, i, p: (i, h)),
+                pl.BlockSpec((1, Q_ROWS, 1), lambda h, i, p: (h, i, 0)),
+            ],
+        ),
+        compiler_params=pltpu.CompilerParams(vmem_limit_bytes=32 * 1024 * 1024),
+        cost_estimate=pl.CostEstimate(
+            flops=4 * pairs * seq * width, transcendentals=pairs * seq * heads, bytes_accessed=8 * pairs * width
+        ),
+        name="attend",
+    )(prefix, queries, keys, values)
+
+
+def attend_back_kernel(
+    tokens, prefix_ref, q_ref, up_ref, k_ref, v_ref, lse_ref, dq_ref, dk_ref, dv_ref, dk_acc, dv_acc
+):
+    tile = pl.program_id(1)
+    rows, keys = q_ref.shape[0], k_ref.shape[0]
+    scale = HEAD_DIM ** (-0.5)
+
+    @pl.when(tile == 0)
+    def _():
+        dk_acc[...] = jnp.zeros_like(dk_acc)
+        dv_acc[...] = jnp.zeros_like(dv_acc)
+
+    scores = lax.dot_general(q_ref[...], k_ref[...], (((1,), (1,)), ((), ())), preferred_element_type=F32)
+    scores = jnp.where(head_mask(tile, rows, tokens, keys, prefix_ref[0]), scores * scale, -jnp.inf)
+    probs = jnp.exp(scores - lse_ref[0])
+    upstream = up_ref[...]
+    grad_probs = lax.dot_general(upstream, v_ref[...], (((1,), (1,)), ((), ())), preferred_element_type=F32)
+    delta = jnp.sum(grad_probs * probs, axis=1, keepdims=True)
+    grad_scores = (probs * (grad_probs - delta)).astype(BF16)
+    dq_ref[...] = (jnp.dot(grad_scores, k_ref[...], preferred_element_type=F32) * scale).astype(BF16)
+    dk_acc[...] += lax.dot_general(grad_scores, q_ref[...], (((0,), (0,)), ((), ())), preferred_element_type=F32)
+    dv_acc[...] += lax.dot_general(
+        probs.astype(BF16), upstream, (((0,), (0,)), ((), ())), preferred_element_type=F32
+    )
+
+    @pl.when(tile == pl.num_programs(1) - 1)
+    def _():
+        dk_ref[...] = (dk_acc[...] * scale).astype(BF16)
+        dv_ref[...] = dv_acc[...].astype(BF16)
+
+
+def attend_back(prefix, queries, upstream, keys, values, lse):
+    pairs, width = queries.shape
+    seq = keys.shape[0]
+    heads = width // HEAD_DIM
+    tiles = pairs // Q_ROWS
+    by_tile = pl.BlockSpec((Q_ROWS, HEAD_DIM), lambda h, i, p: (i, h))
+    by_head = pl.BlockSpec((seq, HEAD_DIM), lambda h, i, p: (0, h))
+    return pl.pallas_call(
+        functools.partial(attend_back_kernel, pairs // 2),
+        out_shape=(
+            jax.ShapeDtypeStruct((pairs, width), BF16),
+            jax.ShapeDtypeStruct((seq, width), BF16),
+            jax.ShapeDtypeStruct((seq, width), BF16),
+        ),
+        grid_spec=pltpu.PrefetchScalarGridSpec(
+            num_scalar_prefetch=1,
+            grid=(heads, tiles),
+            in_specs=[
+                by_tile,
+                by_tile,
+                by_head,
+                by_head,
+                pl.BlockSpec((1, Q_ROWS, 1), lambda h, i, p: (h, i, 0)),
+            ],
+            out_specs=[by_tile, by_head, by_head],
+            scratch_shapes=[pltpu.VMEM((seq, HEAD_DIM), F32), pltpu.VMEM((seq, HEAD_DIM), F32)],
+        ),
+        compiler_params=pltpu.CompilerParams(vmem_limit_bytes=32 * 1024 * 1024),
+        cost_estimate=pl.CostEstimate(
+            flops=10 * pairs * seq * width, transcendentals=pairs * seq * heads, bytes_accessed=8 * pairs * width
+        ),
+        name="attend_back",
+    )(prefix, queries, upstream, keys, values, lse)
+
+
+PLANE = ("expert", "shard")
+GROUP = ("dp", "shard")
+ALL = ("dp", "expert", "shard")
+
+
+def gather_rows(rows, axes):
+    return lax.all_gather(rows, axes, axis=0, tiled=True)
+
+
+def sum_rows(partial, axes):
+    pieces = lax.all_to_all(partial, axes, split_axis=0, concat_axis=0, tiled=True)
+    count = lax.axis_size(axes)
+    return jnp.sum(pieces.reshape(count, -1, partial.shape[1]).astype(F32), axis=0)
+
+
+def exchange(blocks, axes):
+    return lax.all_to_all(blocks, axes, split_axis=0, concat_axis=0, tiled=True)
+
+
 def per_device(
+    tokens,
+    norm_gains,
+    routers,
+    kv_weight,
+    query_weight,
+    output_weight,
+    inner_weight,
+    outer_weight,
+    route_attn,
+    route_mlp,
+    prefix,
+    cotangent,
+):
+    tok = tokens.shape[1]
+    experts = lax.axis_size("expert")
+    depth = lax.axis_size("dp")
+    sides = lax.axis_size("shard")
+    plane = experts * sides
+    group = depth * sides
+    everyone = plane * depth
+    capacity = 5 * tok // (2 * experts)
+    seq = plane * tok
+    qwidth = HEADS * HEAD_DIM
+    own = qwidth // plane
+    half = FF // group
+    my_expert = lax.axis_index("expert")
+
+    inputs = tokens[0].astype(F32)
+    factor_attn = lax.rsqrt(jnp.mean(inputs * inputs, axis=1, keepdims=True) + eps)
+    normed_attn = (inputs * factor_attn * norm_gains[0]).astype(BF16)
+    grad_rows = cotangent[0]
+
+    expert_ids = jnp.arange(experts, dtype=jnp.int32)
+    chosen_attn = (route_attn[0][:, :, None] == expert_ids).astype(F32)
+    chosen_mlp = (route_mlp[0][:, :, None] == expert_ids).astype(F32)
+
+    def keep_of(chosen):
+        flags = jnp.sum(chosen, axis=1)
+        rank = exclusive_count(flags.T).T
+        return jnp.sum(chosen * (rank < capacity).astype(F32)[:, None, :], axis=2)
+
+    keep_attn = keep_of(chosen_attn)
+    keep_mlp = keep_of(chosen_mlp)
+    gate_attn = gates_of(normed_attn, routers[0], chosen_attn)
+    weight_attn = keep_attn * gate_attn
+
+    kv_parts = kv_weight.reshape(-1, 2, plane, own).transpose(2, 0, 1, 3)
+    kv_mine = exchange(kv_parts, PLANE).reshape(-1, 2 * own)
+    kv_mine = gather_rows(kv_mine, "dp")
+    query_parts = query_weight[0].reshape(-1, plane, own).transpose(1, 0, 2)
+    query_mine = exchange(query_parts, PLANE)
+    rows_each = query_parts.shape[1]
+    query_mine = lax.all_gather(query_mine.reshape(experts, sides * rows_each, own), "dp", axis=1, tiled=True)
+    output_all = lax.all_gather(output_weight[0], "dp", axis=0, tiled=False)
+    output_mine = exchange(output_all, "expert")
+
+    normed_seq = gather_rows(normed_attn, PLANE)
+    meta = jnp.concatenate(
+        [weight_attn[:, :, None] * chosen_attn, keep_attn[:, :, None] * chosen_attn], axis=1
+    ).reshape(tok, -1)
+    meta_seq = gather_rows(meta, PLANE).reshape(seq, 2, 2, experts)
+    weigh = meta_seq[:, 0]
+    pick = meta_seq[:, 1]
+
+    kv_seq = matmul(normed_seq, kv_mine).astype(BF16)
+    keys, values = kv_seq[:, :own], kv_seq[:, own:]
+    every_query = jnp.einsum("td,edq->teq", normed_seq, query_mine, preferred_element_type=F32)
+    queries = [
+        sum(pick[:, choice, e, None] * every_query[:, e] for e in range(experts)).astype(BF16) for choice in (0, 1)
+    ]
+    queries = jnp.concatenate(queries, axis=0)
+    attended, lse = attend(prefix, queries, keys, values)
+    pair_attended = attended.reshape(2, seq, own).astype(F32)
+    mixed = jnp.stack(
+        [
+            (weigh[:, 0, e, None] * pair_attended[0] + weigh[:, 1, e, None] * pair_attended[1]).astype(BF16)
+            for e in range(experts)
+        ],
+        axis=1,
+    )
+    attn_part = jnp.einsum("teq,eqd->td", mixed, output_mine, preferred_element_type=F32).astype(BF16)
+    hidden_state = inputs + sum_rows(attn_part, PLANE)
+    factor_mlp = lax.rsqrt(jnp.mean(hidden_state * hidden_state, axis=1, keepdims=True) + eps)
+    normed_mlp = (hidden_state * factor_mlp * norm_gains[1]).astype(BF16)
+    gate_mlp = gates_of(normed_mlp, routers[1], chosen_mlp)
+
+    inner_parts = inner_weight[0].reshape(-1, 2, group, half).transpose(2, 0, 1, 3)
+    inner_mine = exchange(inner_parts, GROUP).reshape(-1, 2 * half)
+    outer_mine = outer_weight[0]
+    gated = jnp.concatenate(
+        [jnp.sum(chosen_mlp, axis=1), jnp.sum(gate_mlp[:, :, None] * chosen_mlp, axis=1)], axis=1
+    )
+    gated_all = gather_rows(gated, ALL)
+    flags = lax.dynamic_index_in_dim(gated_all, my_expert, 1, keepdims=False).reshape(everyone, tok)
+    gate_all = lax.dynamic_index_in_dim(gated_all, my_expert + experts, 1, keepdims=False).reshape(everyone, tok)
+    normed_all = gather_rows(normed_mlp, ALL).reshape(everyone, tok, D)
+    grad_all = gather_rows(grad_rows, ALL).reshape(everyone, tok, D)
+    rank = exclusive_count(flags)
+    slot_ids = jnp.arange(capacity, dtype=F32)
+    place = (rank[:, None, :] == slot_ids[None, :, None]) & (flags[:, None, :] > 0)
+    slot_gate = jnp.sum(jnp.where(place, gate_all[:, None, :], 0.0), axis=2).reshape(-1, 1)
+    place = place.astype(BF16)
+
+    def to_slots(rows):
+        return jnp.einsum("bst,btd->bsd", place, rows, preferred_element_type=F32).astype(BF16).reshape(-1, D)
+
+    def to_tokens(slots):
+        slots = slots.reshape(everyone, capacity, -1)
+        return jnp.einsum("bst,bsd->btd", place, slots, preferred_element_type=F32)
+
+    slots_mlp = to_slots(normed_all)
+    slots_grad = to_slots(grad_all)
+    gate_up = matmul(slots_mlp, inner_mine)
+    gate_part = gate_up[:, :half]
+    up_part = gate_up[:, half:]
+    sigmoid_gate = jax.nn.sigmoid(gate_part)
+    activated = gate_part * sigmoid_gate
+    inner = (activated * up_part).astype(BF16)
+    out_part = (matmul(inner, outer_mine) * slot_gate).astype(BF16)
+    out_part = to_tokens(out_part).astype(BF16).reshape(-1, D)
+    raw_inner = jnp.einsum("rd,fd->rf", slots_grad, outer_mine, preferred_element_type=F32)
+    gate_dot = jnp.sum(raw_inner * inner.astype(F32), axis=1, keepdims=True)
+    grad_inner = raw_inner * slot_gate
+    grad_gate = grad_inner * up_part * (sigmoid_gate * (1.0 + gate_part * (1.0 - sigmoid_gate)))
+    grad_up = grad_inner * activated
+    grad_gate_up = jnp.concatenate([grad_gate, grad_up], axis=1).astype(BF16)
+    scaled_inner = (inner.astype(F32) * slot_gate).astype(BF16)
+    outer_grad = jnp.einsum("rf,rd->fd", scaled_inner, slots_grad, preferred_element_type=F32)
+    inner_grad = jnp.einsum("rd,rf->df", slots_mlp, grad_gate_up, preferred_element_type=F32).astype(BF16)
+    grad_part = jnp.einsum("rf,df->rd", grad_gate_up, inner_mine, preferred_element_type=F32).astype(BF16)
+    grad_part = to_tokens(grad_part).astype(BF16).reshape(-1, D)
+
+    grad_normed_mlp = sum_rows(grad_part, ALL)
+    dot_tokens = jnp.sum(place.astype(F32) * gate_dot.reshape(everyone, capacity, 1), axis=1)
+    dot_mine = lax.all_to_all(dot_tokens, ALL, split_axis=0, concat_axis=0, tiled=True)
+    dot_mine = jnp.sum(dot_mine.reshape(depth, experts, sides, tok), axis=(0, 2))
+    grad_gate_mlp = keep_mlp * jnp.sum(chosen_mlp * dot_mine.T[:, None, :], axis=2)
+    result = hidden_state + sum_rows(out_part, ALL)
+    output = result.astype(BF16)[None]
+    inner_grad = inner_grad.reshape(group, -1, 2 * half)
+    inner_grad = exchange(inner_grad, GROUP)
+    inner_grad = inner_grad.reshape(group, -1, 2, half).transpose(1, 2, 0, 3).reshape(-1, 2 * FF).astype(F32)
+
+    router_grad_mlp, router_part_mlp = router_back(
+        gate_mlp, grad_gate_mlp, chosen_mlp, normed_mlp, routers[1]
+    )
+    grad_normed_mlp = grad_normed_mlp + router_part_mlp
+    grad_hidden, gain_grad_mlp = norm_back(hidden_state, factor_mlp, norm_gains[1], grad_normed_mlp)
+    grad_hidden = grad_hidden + grad_rows.astype(F32)
+
+    hidden_seq = gather_rows(grad_hidden.astype(BF16), PLANE)
+    raw_attended = jnp.einsum("td,eqd->teq", hidden_seq, output_mine, preferred_element_type=F32)
+    raw_pair = [sum(pick[:, choice, e, None] * raw_attended[:, e] for e in range(experts)) for choice in (0, 1)]
+    gate_dots = jnp.stack([jnp.sum(raw_pair[c] * pair_attended[c], axis=1) for c in (0, 1)], axis=1)
+    weight_seq = jnp.sum(weigh, axis=2)
+    upstream = jnp.concatenate([(weight_seq[:, c, None] * raw_pair[c]).astype(BF16) for c in (0, 1)], axis=0)
+    grad_queries, grad_keys, grad_values = attend_back(prefix, queries, upstream, keys, values, lse)
+    pair_grads = grad_queries.reshape(2, seq, own)
+    spread = jnp.stack(
+        [
+            (pick[:, 0, e, None] * pair_grads[0] + pick[:, 1, e, None] * pair_grads[1]).astype(BF16)
+            for e in range(experts)
+        ],
+        axis=1,
+    )
+    row_part = jnp.einsum("teq,edq->td", spread, query_mine, preferred_element_type=F32)
+    grad_kv = jnp.concatenate([grad_keys, grad_values], axis=1)
+    row_part = row_part + jnp.einsum("tk,dk->td", grad_kv, kv_mine, preferred_element_type=F32)
+    grad_normed_attn = sum_rows(row_part.astype(BF16), PLANE)
+    dots_mine = sum_rows(gate_dots, PLANE)
+    grad_gate_attn = keep_attn * dots_mine
+
+    output_grad = jnp.einsum("teq,td->eqd", mixed, hidden_seq, preferred_element_type=F32).astype(BF16)
+    output_grad = exchange(output_grad, "expert")
+    output_grad = sum_rows(output_grad.reshape(depth * own, D), "dp")
+    query_grad = jnp.einsum("td,teq->deq", normed_seq, spread, preferred_element_type=F32).astype(BF16)
+    kv_grad = jnp.einsum("td,tk->dk", normed_seq, grad_kv, preferred_element_type=F32).astype(BF16)
+    query_grad = sum_rows(query_grad.reshape(D, -1), "dp").astype(BF16)
+    kv_grad = sum_rows(kv_grad, "dp").astype(BF16)
+    query_grad = query_grad.reshape(sides, rows_each, experts, own).transpose(2, 0, 1, 3).reshape(plane, rows_each, own)
+    query_grad = exchange(query_grad, PLANE).transpose(1, 0, 2).reshape(rows_each, qwidth).astype(F32)
+    kv_grad = exchange(kv_grad.reshape(plane, -1, 2 * own), PLANE)
+    kv_grad = kv_grad.reshape(plane, -1, 2, own).transpose(1, 2, 0, 3).reshape(-1, 2 * qwidth).astype(F32)
+
+    router_grad_attn, router_part_attn = router_back(
+        gate_attn, grad_gate_attn, chosen_attn, normed_attn, routers[0]
+    )
+    grad_normed_attn = grad_normed_attn + router_part_attn
+    grad_inputs, gain_grad_attn = norm_back(inputs, factor_attn, norm_gains[0], grad_normed_attn)
+    grad_inputs = grad_inputs + grad_hidden
+    gain_grad, router_grad = lax.psum(
+        (
+            jnp.stack([gain_grad_attn, gain_grad_mlp]),
+            jnp.stack([router_grad_attn, router_grad_mlp]),
+        ),
+        ("dp", "expert", "shard"),
+    )
+    return (
+        output,
+        grad_inputs[None],
+        gain_grad,
+        router_grad,
+        kv_grad,
+        query_grad[None],
+        output_grad[None],
+        inner_grad[None],
+        outer_grad[None],
+    )
+
+
+def per_device_gathered(
     tokens,
     norm_gains,
     routers,
@@ -337,8 +700,10 @@
 
 
 def solution(mesh):
+    plane = mesh.shape["expert"] * mesh.shape["shard"]
+    fits = HEADS % plane == 0
     return jax.shard_map(
-        per_device,
+        per_device if fits else per_device_gathered,
         mesh=mesh,
         in_specs=(
             P("dp", ("expert", "shard"), None),

time: 4450 us -> 2160 us (0.49)
  waiting for transfers between devices: 3700 us -> 1390 us
  matrix products: 432 us -> 220 us
  blocking collectives: 104 us -> 261 us
  loops' own time: 53.5 us -> 0 us
    reduce_scatter x5 -> x0, waiting for transfers between devices: 1270 us -> none  [the longest x1 710 us: per_device(): lax.psum_scatter(jnp.einsum('td,tk->dk', piece, grad_keys, preferred_elem...]
    all_gather x6 -> x7, waiting for transfers between devices: 1500 us -> 287 us  [the longest x5 180 us: gather_rows(): return lax.all_gather(rows, axes, axis=0, tiled=True)]
    all_to_all x9 -> x13, waiting for transfers between devices: 87.8 us -> 1040 us  [the longest x7 736 us: sum_rows(): lax.all_to_all(partial, axes, split_axis=0, concat_axis=0, tiled=True)]
    unnamed x14 -> x8, waiting for transfers between devices: 726 us -> 1.31 us
    dot_general x145 -> x28, matrix products: 432 us -> 220 us  [the longest x3 41.4 us: matmul(): return jnp.dot(first, second, preferred_element_type=F32)]
    all_gather x0 -> x2, blocking collectives: none -> 82.9 us  [gather_rows(): return lax.all_gather(rows, axes, axis=0, tiled=True)]
    all_to_all x3 -> x4, blocking collectives: 64.2 us -> 127 us  [the longest x1 78.1 us: sum_rows(): lax.all_to_all(partial, axes, split_axis=0, concat_axis=0, tiled=True)]
    psum x1, waiting for transfers between devices: 116 us -> 61.2 us  [per_device(): lax.psum((jnp.stack([gain_grad_attn, gain_grad_mlp]), jnp.stack([router_g...]
  transfers between devices with their start and end apart: 22 -> 21, of which waited for: 19 -> 14; matrix products, arithmetic and copies ran while one was open for 7% -> 15% of each run, Pallas kernels for 0% -> 2%
where the time goes in v1:
time: 2160 us
  waiting for transfers between devices  1390 us (64%)
  blocking collectives  261 us (12%)
  matrix products  220 us (10%)
  local copies, waits for them, and re-layouts  101 us (5%)
  other arithmetic  69.8 us (3%)
  starting transfers between devices  63.8 us (3%)
  Pallas kernels  36 us (2%)
    all_to_all x7, waiting for transfers between devices, sum_rows(): lax.all_to_all(partial, axes, split_axis=0, concat_axis=0, tiled=True)  736 us
    all_to_all x5, waiting for transfers between devices, exchange(): return lax.all_to_all(blocks, axes, split_axis=0, concat_axis=0, tiled=True)  302 us
    all_gather x5, waiting for transfers between devices, gather_rows(): return lax.all_gather(rows, axes, axis=0, tiled=True)  180 us
    all_gather x2, blocking collectives, gather_rows(): return lax.all_gather(rows, axes, axis=0, tiled=True)  82.9 us
    all_to_all x1, blocking collectives, sum_rows(): lax.all_to_all(partial, axes, split_axis=0, concat_axis=0, tiled=True)  78.1 us
    all_gather x1, waiting for transfers between devices, per_device(): lax.all_gather(query_mine.reshape(experts, sides * rows_each, own), 'dp',...  75.7 us
    psum x1, waiting for transfers between devices, per_device(): lax.psum((jnp.stack([gain_grad_attn, gain_grad_mlp]), jnp.stack([router_g...  61.2 us
    psum x1, blocking collectives, per_device(): lax.psum((jnp.stack([gain_grad_attn, gain_grad_mlp]), jnp.stack([router_g...  51.7 us
  transfers between devices with their start and end apart: 21, of which 14 were waited for; matrix products, arithmetic and copies ran while one was open for 15% of the time, Pallas kernels for 2%

profile of v1, /device:TPU:0, one launch (start us, length us, event | category | flops | bytes accessed | tf_op | source)
XLA Modules:
  0.0 2156.8 jit_solution(18070534486818933800)
XLA Ops:
  9.8 19.5 all_to_all.109
  32.3 11.3 all_to_all.110
  47.3 13.9 all_gather.27
  62.0 31.1 %all-gather.15.cloned.1.call-done = bf16[4,256,2048]{2,1,0:T(8,128)(2,1)} async-done(((bf16[1,256,2048]{2,1,0:T(8,128)(2,1)}), bf16[4,256,2048]{2,1,0:T(8,128)(2,1)}) %all-gather.15.cloned.1.call-update) | async-done | bytes 4194320 | tf_op jit(solution)/shard_map/all_gather | solution.py:281
  98.2 75.7 %all-gather.11.cloned.1.call-done = bf16[4,2048,256]{2,1,0:T(8,128)(2,1)} async-done(((bf16[4,512,256]{2,1,0:T(8,128)(2,1)}), bf16[4,2048,256]{2,1,0:T(8,128)(2,1)}) %all-gather.11.cloned.1.call-update) | async-done | bytes 4194320 | tf_op jit(solution)/shard_map/all_gather | solution.py:280
  173.9 37.0 %all-gather.9.cloned.1.call-done = bf16[1024,2048]{1,0:T(8,128)(2,1)} async-done(((bf16[128,2048]{1,0:T(8,128)(2,1)}), bf16[1024,2048]{1,0:T(8,128)(2,1)}) %all-gather.9.cloned.1.call-update) | async-done | bytes 4194320 | tf_op jit(solution)/shard_map/all_gather | solution.py:214
  210.9 7.5 fusion.10
  221.0 37.5 %all-gather.13.cloned.1.call-done = bf16[2048,512]{1,0:T(8,128)(2,1)} async-done(((bf16[512,512]{1,0:T(8,128)(2,1)}), bf16[2048,512]{1,0:T(8,128)(2,1)}) %all-gather.13.cloned.1.call-update) | async-done | bytes 2097168 | tf_op jit(solution)/shard_map/all_gather | solution.py:214
  264.0 15.7 attend.1
  284.3 7.3 bitcast_convert_fusion
  291.6 78.1 %all_to_all.111 = bf16[8,128,2048]{2,1,0:T(8,128)(2,1)S(1)} all-to-all(bf16[8,128,2048]{2,1,0:T(8,128)(2,1)S(1)} %bitcast.355), channel_id=1, replica_groups=mesh['dp'=4,'expert'=4,'shard'=2] {'expert','shard'}, dimensions={0} | all-to-all | bytes 8388608 | tf_op jit(solution)/shard_map/all_to_all | solution.py:218
  372.4 8.2 copy.85
  392.3 165.6 %all-to-all-done.4 = bf16[8,256,2,704]{1,3,2,0:T(8,128)(2,1)} async-done(((bf16[8,256,2,704]{1,3,2,0:T(8,128)(2,1)}), bf16[8,256,2,704]{1,3,2,0:T(8,128)(2,1)}, u32[]{:S(2)}, u32[]{:S(2)}) %all-to-all-start.4) | async-done | bytes 5767200 | tf_op jit(solution)/shard_map/all_to_all | solution.py:224
  570.2 69.0 %all_gather.32 = f32[4096,8]{0,1:T(8,128)S(1)} all-gather(f32[128,8]{0,1:T(8,128)S(1)} %pad_maximum_fusion.15), channel_id=1, replica_groups=mesh['dp'=4,'expert'=4,'shard'=2] {'dp','expert','shard'}, dimensions={0}, use_global_device_ids=true | all-gather | bytes 135168 | tf_op jit(solution)/shard_map/all_gather | solution.py:214
  639.6 12.6 convolution_convert_fusion.4
  652.2 12.7 convolution_convert_fusion.5
  664.9 23.1 %fusion.117 = f32[2560,1408]{0,1:T(8,128)} fusion(bf16[2560,2048]{1,0:T(8,128)(2,1)} %bitcast.344, bf16[2048,1408]{0,1:T(8,128)(2,1)} %bitcast.351), kind=kOutput, calls=%fused_computation.224 | convolution fusion | flops 14763950080 | bytes 30670848 | tf_op jit(solution)/shard_map/dot_general | solution.py:22
  688.0 14.2 fusion.1
  706.3 11.2 multiply_convert_fusion.2
  717.4 20.8 convolution_convert_fusion.3
  738.3 8.3 copy.99
  752.8 22.9 %convolution_convert_fusion.2 = bf16[2560,2048]{1,0:T(8,128)(2,1)} fusion(bf16[2048,1408]{0,1:T(8,128)(2,1)} %bitcast.352, bf16[2560,704]{0,1:T(8,128)(2,1)} %get-tuple-element.80, bf16[2560,704]{0,1:T(8,128)(2,1)} %copy-done.26), kind=kOutput, calls=%fused_computation.6 | convolution fusion | flops 14783610880 | bytes 23461888 | tf_op jit(solution)/shard_map/rf,df->rd/dot_general | solution.py:357
  775.7 10.6 convolution_convert_fusion
  786.3 93.7 %all-to-all-done.16 = bf16[8,256,1408]{1,2,0:T(8,128)(2,1)} async-done(((bf16[8,256,1408]{1,2,0:T(8,128)(2,1)}), bf16[8,256,1408]{1,2,0:T(8,128)(2,1)}, u32[]{:S(2)}, u32[]{:S(2)}) %all-to-all-start.16) | async-done | bytes 5767200 | tf_op jit(solution)/shard_map/all_to_all | solution.py:224
  884.2 13.0 multiply_convert_fusion
  897.2 10.6 convolution_convert_fusion.1
  907.8 346.9 %all-to-all-done.6 = bf16[32,128,2048]{2,1,0:T(8,128)(2,1)} async-done(((bf16[32,128,2048]{2,1,0:T(8,128)(2,1)}), bf16[32,128,2048]{2,1,0:T(8,128)(2,1)}, u32[]{:S(2)}, u32[]{:S(2)}) %all-to-all-start.6) | async-done | bytes 16777248 | tf_op jit(solution)/shard_map/all_to_all | solution.py:218
  1254.7 8.2 all-to-all-start.5
  1263.4 7.4 convert_reduce_fusion
  1273.6 105.5 %all-gather.19.cloned.1.call-done = bf16[1024,2048]{1,0:T(8,128)(2,1)} async-done(((bf16[128,2048]{1,0:T(8,128)(2,1)}), bf16[1024,2048]{1,0:T(8,128)(2,1)}) %all-gather.19.cloned.1.call-update) | async-done | bytes 4194320 | tf_op jit(solution)/shard_map/all_gather | solution.py:214
  1379.2 7.6 fusion.6
  1391.1 20.3 attend_back.1
  1411.5 221.9 %all-to-all-done.5 = bf16[32,128,2048]{2,1,0:T(8,128)(2,1)} async-done(((bf16[32,128,2048]{2,1,0:T(8,128)(2,1)}), bf16[32,128,2048]{2,1,0:T(8,128)(2,1)}, u32[]{:S(2)}, u32[]{:S(2)}) %all-to-all-start.5) | async-done | bytes 16777248 | tf_op jit(solution)/shard_map/all_to_all | solution.py:218
  1647.4 9.1 fusion.15
  1656.5 39.9 %all-to-all-done.10 = bf16[4,512,512]{2,1,0:T(8,128)(2,1)} async-done(((bf16[4,512,512]{2,1,0:T(8,128)(2,1)}), bf16[4,512,512]{2,1,0:T(8,128)(2,1)}, u32[]{:S(2)}, u32[]{:S(2)}) %all-to-all-start.10) | async-done | bytes 2097184 | tf_op jit(solution)/shard_map/all_to_all | solution.py:218
  1706.6 43.0 %all-to-all-done.14 = bf16[4,256,2048]{2,1,0:T(8,128)(2,1)} async-done(((bf16[4,256,2048]{2,1,0:T(8,128)(2,1)}), bf16[4,256,2048]{2,1,0:T(8,128)(2,1)}, u32[]{:S(2)}, u32[]{:S(2)}) %all-to-all-start.14) | async-done | bytes 4194336 | tf_op jit(solution)/shard_map/all_to_all | solution.py:224
  1760.3 17.1 copy.95
  1777.4 7.7 all_to_all.86
  1801.7 83.5 %all-to-all-done.12 = bf16[4,512,1024]{2,1,0:T(8,128)(2,1)} async-done(((bf16[4,512,1024]{2,1,0:T(8,128)(2,1)}), bf16[4,512,1024]{2,1,0:T(8,128)(2,1)}, u32[]{:S(2)}, u32[]{:S(2)}) %all-to-all-start.12) | async-done | bytes 4194336 | tf_op jit(solution)/shard_map/all_to_all | solution.py:218
  1894.0 44.0 %all-to-all-done.8 = bf16[8,128,2048]{2,1,0:T(8,128)(2,1)} async-done(((bf16[8,128,2048]{2,1,0:T(8,128)(2,1)}), bf16[8,128,2048]{2,1,0:T(8,128)(2,1)}, u32[]{:S(2)}, u32[]{:S(2)}) %all-to-all-start.8) | async-done | bytes 4194336 | tf_op jit(solution)/shard_map/all_to_all | solution.py:218
  1938.0 17.5 all_to_all.112
  1960.5 13.3 convolution_bitcast_fusion
  1974.1 8.3 convert_bitcast_fusion
  1982.4 9.6 copy.100
  1992.0 11.9 copy.102
  2003.9 7.2 convert_reduce_fusion.1
  2022.5 51.7 %psum.14 = f32[2,2048]{1,0:T(2,128)} all-reduce(f32[2,2048]{1,0:T(2,128)S(1)} %pad_maximum_fusion.12), channel_id=1, replica_groups=mesh['dp'=4,'expert'=4,'shard'=2] {'dp','expert','shard'}, use_global_device_ids=true, to_apply=%region_34.35 | all-reduce | flops 4096 | bytes 32768 | tf_op jit(solution)/shard_map/psum | solution.py:418
  2086.7 61.2 %all-reduce.2.cloned.1.call-done = f32[2,2048,4]{1,2,0:T(4,128)} async-done(((f32[2,2048,4]{1,2,0:T(4,128)}), f32[2,2048,4]{1,2,0:T(4,128)}) %all-reduce.2.cloned.1.call-update) | async-done | bytes 65552 | tf_op jit(solution)/shard_map/psum | solution.py:418
  (287 shorter events, 165.8 us)
Async XLA Ops:
  7.2 680.8 %copy-start = (bf16[1,704,2048]{2,1,0:T(8,128)(2,1)S(1)}, bf16[1,704,2048]{2,1,0:T(8,128)(2,1)}, u32[]{:S(2)}) copy-start(bf16[1,704,2048]{2,1,0:T(8,128)(2,1)} %param.19) | copy-start | bytes 8650756
  7.2 85.9 %all-gather.15.cloned.1.call-start = ((), (), s32[]{:S(2)}) async-start(), calls=%async_computation.20 | async-start | bytes 5242880 | tf_op jit(solution)/shard_map/all_gather | solution.py:281
  7.9 166.0 %all-gather.11.cloned.1.call-start = ((), (), s32[]{:S(2)}) async-start(), calls=%async_computation.18 | async-start | bytes 5242880 | tf_op jit(solution)/shard_map/all_gather | solution.py:280
  29.4 181.5 %all-gather.9.cloned.1.call-start = ((), (), s32[]{:S(2)}) async-start(), calls=%async_computation.17 | async-start | bytes 4718592 | tf_op jit(solution)/shard_map/all_gather | solution.py:214
  29.7 539.2 %copy-start.32 = (f32[1,2048]{1,0:T(1,128)}, f32[1,2048]{1,0:T(1,128)S(1)}, u32[]{:S(2)}) copy-start(f32[1,2048]{1,0:T(1,128)S(1)} %get-tuple-element.112) | copy-start | bytes 24580
  30.7 227.9 %all-gather.13.cloned.1.call-start = ((), (), s32[]{:S(2)}) async-start(), calls=%async_computation.19 | async-start | bytes 2621440 | tf_op jit(solution)/shard_map/all_gather | solution.py:214
  44.6 595.0 %all-gather.21.cloned.1.call-start = ((), (), s32[]{:S(2)}) async-start(), calls=%async_computation.24 | async-start | bytes 17301504 | tf_op jit(solution)/shard_map/all_gather | solution.py:214
  61.9 156.5 %copy-start.40 = (f32[1024,1,1]{0,2,1:T(1,128)}, f32[1024,1,1]{0,2,1:T(1,128)S(1)}, u32[]{:S(2)}) copy-start(f32[1024,1,1]{0,2,1:T(1,128)S(1)} %get-tuple-element.121) | copy-start | bytes 12292
  61.9 156.5 %copy-start.42 = (f32[1024,1,1]{0,2,1:T(1,128)}, f32[1024,1,1]{0,2,1:T(1,128)S(1)}, u32[]{:S(2)}) copy-start(f32[1024,1,1]{0,2,1:T(1,128)S(1)} %get-tuple-element.122) | copy-start | bytes 12292
  61.9 156.5 %copy-start.44 = (f32[1024,1,1]{0,2,1:T(1,128)}, f32[1024,1,1]{0,2,1:T(1,128)S(1)}, u32[]{:S(2)}) copy-start(f32[1024,1,1]{0,2,1:T(1,128)S(1)} %get-tuple-element.123) | copy-start | bytes 12292
  61.9 156.5 %copy-start.46 = (f32[1024,1,1]{0,2,1:T(1,128)}, f32[1024,1,1]{0,2,1:T(1,128)S(1)}, u32[]{:S(2)}) copy-start(f32[1024,1,1]{0,2,1:T(1,128)S(1)} %get-tuple-element.124) | copy-start | bytes 12292
  61.9 156.5 %copy-start.48 = (f32[1024,1,1]{0,2,1:T(1,128)}, f32[1024,1,1]{0,2,1:T(1,128)S(1)}, u32[]{:S(2)}) copy-start(f32[1024,1,1]{0,2,1:T(1,128)S(1)} %get-tuple-element.125) | copy-start | bytes 12292
  61.9 156.5 %copy-start.50 = (f32[1024,1,1]{0,2,1:T(1,128)}, f32[1024,1,1]{0,2,1:T(1,128)S(1)}, u32[]{:S(2)}) copy-start(f32[1024,1,1]{0,2,1:T(1,128)S(1)} %get-tuple-element.126) | copy-start | bytes 12292
  61.9 156.5 %copy-start.52 = (f32[1024,1,1]{0,2,1:T(1,128)}, f32[1024,1,1]{0,2,1:T(1,128)S(1)}, u32[]{:S(2)}) copy-start(f32[1024,1,1]{0,2,1:T(1,128)S(1)} %get-tuple-element.127) | copy-start | bytes 12292
  61.9 156.5 %copy-start.54 = (f32[1024,1,1]{0,2,1:T(1,128)}, f32[1024,1,1]{0,2,1:T(1,128)S(1)}, u32[]{:S(2)}) copy-start(f32[1024,1,1]{0,2,1:T(1,128)S(1)} %get-tuple-element.128) | copy-start | bytes 12292
  93.1 191.2 %all-to-all-start.2 = ((bf16[4,256,2048]{2,1,0:T(8,128)(2,1)}), bf16[4,256,2048]{2,1,0:T(8,128)(2,1)}, u32[]{:S(2)}, u32[]{:S(2)}) async-start(bf16[4,256,2048]{2,1,0:T(8,128)(2,1)} %all-gather.15.cloned.1.call-done), calls=%async_computation.2 | async-start | bytes 8388608 | tf_op jit(solution)/shard_map/all_to_all | solution.py:224
  98.0 554.2 %all-gather.17.cloned.1.call-start = ((), (), s32[]{:S(2)}) async-start(), calls=%async_computation.21 | async-start | bytes 17301504 | tf_op jit(solution)/shard_map/all_gather | solution.py:214
  370.6 198.2 %copy-start.68 = (f32[128]{0:T(128)}, f32[128]{0:T(128)S(1)}, u32[]{:S(2)}) copy-start(f32[128]{0:T(128)S(1)} %add_rsqrt_fusion) | copy-start | bytes 1540
  386.5 171.3 %all-to-all-start.4 = ((bf16[8,256,2,704]{1,3,2,0:T(8,128)(2,1)}), bf16[8,256,2,704]{1,3,2,0:T(8,128)(2,1)}, u32[]{:S(2)}, u32[]{:S(2)}) async-start(bf16[8,256,2,704]{1,3,2,0:T(8,128)(2,1)} %copy.86), calls=%async_computation.4 | async-start | bytes 11534336 | tf_op jit(solution)/shard_map/all_to_all | solution.py:224
  703.5 43.1 %all-to-all-start.7 = ((f32[32,1,128]{2,1,0:T(1,128)}), f32[32,1,128]{2,1,0:T(1,128)S(1)}, u32[]{:S(2)}, u32[]{:S(2)}) async-start(f32[32,1,128]{2,1,0:T(1,128)} %bitcast.53), calls=%async_computation.7 | async-start | bytes 32768 | tf_op jit(solution)/shard_map/all_to_all | solution.py:362
  746.6 133.4 %all-to-all-start.16 = ((bf16[8,256,1408]{1,2,0:T(8,128)(2,1)}), bf16[8,256,1408]{1,2,0:T(8,128)(2,1)}, u32[]{:S(2)}, u32[]{:S(2)}) async-start(bf16[8,256,1408]{1,2,0:T(8,128)(2,1)} %copy.99), calls=%async_computation.16 | async-start | bytes 11534336 | tf_op jit(solution)/shard_map/all_to_all | solution.py:224
  880.0 374.7 %all-to-all-start.6 = ((bf16[32,128,2048]{2,1,0:T(8,128)(2,1)}), bf16[32,128,2048]{2,1,0:T(8,128)(2,1)}, u32[]{:S(2)}, u32[]{:S(2)}) async-start(bf16[32,128,2048]{2,1,0:T(8,128)(2,1)} %convolution_convert_fusion), calls=%async_computation.6 | async-start | bytes 33554432 | tf_op jit(solution)/shard_map/all_to_all | solution.py:218
  907.8 355.2 %copy-start.72 = (f32[128,4]{0,1:T(4,128)S(1)}, f32[128,4]{0,1:T(4,128)}, u32[]{:S(2)}) copy-start(f32[128,4]{0,1:T(4,128)} %copy-done.71) | copy-start | bytes 6148
  907.8 355.4 %copy-start.61 = (s32[1,128,2]{1,2,0:T(2,128)S(1)}, s32[1,128,2]{1,2,0:T(2,128)}, u32[]{:S(2)}) copy-start(s32[1,128,2]{1,2,0:T(2,128)} %param.21) | copy-start | bytes 3076
  907.8 355.4 %copy-start.57 = (f32[128,2]{0,1:T(2,128)S(1)}, f32[128,2]{0,1:T(2,128)}, u32[]{:S(2)}) copy-start(f32[128,2]{0,1:T(2,128)} %copy-done.56) | copy-start | bytes 3076
  907.8 355.5 %copy-start.67 = (f32[128]{0:T(128)S(1)}, f32[128]{0:T(128)}, u32[]{:S(2)}) copy-start(f32[128]{0:T(128)} %copy-done.66) | copy-start | bytes 1540
  907.8 355.5 %copy-start.74 = (f32[128]{0:T(128)S(1)}, f32[128]{0:T(128)}, u32[]{:S(2)}) copy-start(f32[128]{0:T(128)} %copy-done.73) | copy-start | bytes 1540
  1254.7 378.6 %all-to-all-start.5 = ((bf16[32,128,2048]{2,1,0:T(8,128)(2,1)}), bf16[32,128,2048]{2,1,0:T(8,128)(2,1)}, u32[]{:S(2)}, u32[]{:S(2)}) async-start(bf16[32,128,2048]{2,1,0:T(8,128)(2,1)} %convolution_convert_fusion.1), calls=%async_computation.5 | async-start | bytes 33554432 | tf_op jit(solution)/shard_map/all_to_all | solution.py:218
  1263.0 116.2 %all-gather.19.cloned.1.call-start = ((), (), s32[]{:S(2)}) async-start(), calls=%async_computation.22 | async-start | bytes 4718592 | tf_op jit(solution)/shard_map/all_gather | solution.py:214
  1273.5 113.2 %copy-start.19 = (f32[2048,256]{1,0:T(8,128)S(1)}, f32[2048,256]{1,0:T(8,128)}, u32[]{:S(2)}) copy-start(f32[2048,256]{1,0:T(8,128)} %copy-done.18) | copy-start | bytes 6291460
  1273.6 113.2 %copy-start.41 = (f32[1024,1,1]{0,2,1:T(1,128)S(1)}, f32[1024,1,1]{0,2,1:T(1,128)}, u32[]{:S(2)}) copy-start(f32[1024,1,1]{0,2,1:T(1,128)} %copy-done.40) | copy-start | bytes 12292
  1273.6 113.2 %copy-start.43 = (f32[1024,1,1]{0,2,1:T(1,128)S(1)}, f32[1024,1,1]{0,2,1:T(1,128)}, u32[]{:S(2)}) copy-start(f32[1024,1,1]{0,2,1:T(1,128)} %copy-done.42) | copy-start | bytes 12292
  1273.6 113.2 %copy-start.45 = (f32[1024,1,1]{0,2,1:T(1,128)S(1)}, f32[1024,1,1]{0,2,1:T(1,128)}, u32[]{:S(2)}) copy-start(f32[1024,1,1]{0,2,1:T(1,128)} %copy-done.44) | copy-start | bytes 12292
  1273.6 113.2 %copy-start.47 = (f32[1024,1,1]{0,2,1:T(1,128)S(1)}, f32[1024,1,1]{0,2,1:T(1,128)}, u32[]{:S(2)}) copy-start(f32[1024,1,1]{0,2,1:T(1,128)} %copy-done.46) | copy-start | bytes 12292
  1273.6 113.2 %copy-start.49 = (f32[1024,1,1]{0,2,1:T(1,128)S(1)}, f32[1024,1,1]{0,2,1:T(1,128)}, u32[]{:S(2)}) copy-start(f32[1024,1,1]{0,2,1:T(1,128)} %copy-done.48) | copy-start | bytes 12292
  1273.6 113.2 %copy-start.51 = (f32[1024,1,1]{0,2,1:T(1,128)S(1)}, f32[1024,1,1]{0,2,1:T(1,128)}, u32[]{:S(2)}) copy-start(f32[1024,1,1]{0,2,1:T(1,128)} %copy-done.50) | copy-start | bytes 12292
  1273.6 113.2 %copy-start.53 = (f32[1024,1,1]{0,2,1:T(1,128)S(1)}, f32[1024,1,1]{0,2,1:T(1,128)}, u32[]{:S(2)}) copy-start(f32[1024,1,1]{0,2,1:T(1,128)} %copy-done.52) | copy-start | bytes 12292
  1273.6 113.2 %copy-start.55 = (f32[1024,1,1]{0,2,1:T(1,128)S(1)}, f32[1024,1,1]{0,2,1:T(1,128)}, u32[]{:S(2)}) copy-start(f32[1024,1,1]{0,2,1:T(1,128)} %copy-done.54) | copy-start | bytes 12292
  1411.5 225.2 %copy-start.34 = (bf16[1024,512]{1,0:T(8,128)(2,1)}, bf16[1024,512]{1,0:T(8,128)(2,1)S(1)}, u32[]{:S(2)}) copy-start(bf16[1024,512]{1,0:T(8,128)(2,1)S(1)} %constant_dynamic-update-slice_fusion) | copy-start | bytes 3145732
  1633.3 9.2 all-to-all-start.9
  1642.6 53.9 %all-to-all-start.10 = ((bf16[4,512,512]{2,1,0:T(8,128)(2,1)}), bf16[4,512,512]{2,1,0:T(8,128)(2,1)}, u32[]{:S(2)}, u32[]{:S(2)}) async-start(bf16[4,512,512]{2,1,0:T(8,128)(2,1)} %bitcast.364), calls=%async_computation.10 | async-start | bytes 4194304 | tf_op jit(solution)/shard_map/all_to_all | solution.py:218
  1696.5 53.1 %all-to-all-start.14 = ((bf16[4,256,2048]{2,1,0:T(8,128)(2,1)}), bf16[4,256,2048]{2,1,0:T(8,128)(2,1)}, u32[]{:S(2)}, u32[]{:S(2)}) async-start(bf16[4,256,2048]{2,1,0:T(8,128)(2,1)} %fusion.15), calls=%async_computation.14 | async-start | bytes 8388608 | tf_op jit(solution)/shard_map/all_to_all | solution.py:224
  1749.6 35.6 %all-to-all-start.11 = ((bf16[8,64,512]{2,1,0:T(8,128)(2,1)}), bf16[8,64,512]{2,1,0:T(8,128)(2,1)S(1)}, u32[]{:S(2)}, u32[]{:S(2)}) async-start(bf16[8,64,512]{2,1,0:T(8,128)(2,1)} %bitcast.77), calls=%async_computation.11 | async-start | bytes 1048576 | tf_op jit(solution)/shard_map/all_to_all | solution.py:224
  1785.9 99.2 %all-to-all-start.12 = ((bf16[4,512,1024]{2,1,0:T(8,128)(2,1)}), bf16[4,512,1024]{2,1,0:T(8,128)(2,1)}, u32[]{:S(2)}, u32[]{:S(2)}) async-start(bf16[4,512,1024]{2,1,0:T(8,128)(2,1)} %all_to_all.86), calls=%async_computation.12 | async-start | bytes 8388608 | tf_op jit(solution)/shard_map/all_to_all | solution.py:218
  1885.2 52.8 %all-to-all-start.8 = ((bf16[8,128,2048]{2,1,0:T(8,128)(2,1)}), bf16[8,128,2048]{2,1,0:T(8,128)(2,1)}, u32[]{:S(2)}, u32[]{:S(2)}) async-start(bf16[8,128,2048]{2,1,0:T(8,128)(2,1)} %bitcast.354), calls=%async_computation.8 | async-start | bytes 8388608 | tf_op jit(solution)/shard_map/all_to_all | solution.py:218
  1955.5 126.7 %all-to-all-start.15 = ((bf16[4,256,2048]{2,1,0:T(8,128)(2,1)}), bf16[4,256,2048]{2,1,0:T(8,128)(2,1)}, u32[]{:S(2)}, u32[]{:S(2)}) async-start(bf16[4,256,2048]{2,1,0:T(8,128)(2,1)} %all-to-all-done.14), calls=%async_computation.15 | async-start | bytes 8388608 | tf_op jit(solution)/shard_map/all_to_all | solution.py:218
  1960.4 187.5 %all-reduce.2.cloned.1.call-start = ((), (), s32[]{:S(2)}) async-start(), calls=%async_computation.23 | async-start | bytes 131072 | tf_op jit(solution)/shard_map/psum | solution.py:418
  2079.2 70.3 %copy-start.1 = (bf16[1,704,2048]{2,1,0:T(8,128)(2,1)S(1)}, bf16[1,704,2048]{2,1,0:T(8,128)(2,1)}, u32[]{:S(2)}) copy-start(bf16[1,704,2048]{2,1,0:T(8,128)(2,1)} %param.19) | copy-start | bytes 8650756
  (51 other events, 638.4 us)
Sparse Core Ops, SparseCore 0:
  9.6 83.4 all-gather.14
  94.6 79.2 all-gather.10
  175.8 35.0 all-gather.8
  212.9 45.6 all-gather.12
  261.3 144.1 all-gather.20
  408.2 200.5 all-gather.16
  1273.6 105.5 all-gather.18
  2013.3 134.5 all-reduce.1
